TPU v7x, 512 devices: a whole 4x4x16 slice. The times are simulated.
512 devices in a mesh: outer: 32 (over y, z_hi, core), inner: 16 (over z_lo, x).
Axes of the slice: x: 4, y: 4, z: 16 (z_hi: 4, z_lo: 4; z = z_hi * 4 + z_lo), core: 2. Of those that a mesh axis runs over, the one named last changes fastest.
Arguments:
- group_latents: bfloat16 [65536, 1024], P(('outer', 'inner')), may hold values from -6 to 6
- slot_ids: int32 [32, 16], P('outer', 'inner'), may hold values from 0 to 15, each once within a row
- slot_embed: bfloat16 [16, 1024], replicated, may hold values from -6 to 6
- merge_latents: bfloat16 [128, 2048], replicated, may hold values from -6 to 6
- query_weight: bfloat16 [2048, 2048], P(None, 'inner'), may hold values from -0.125 to 0.125
- key_weight: bfloat16 [1024, 2048], P(None, 'inner'), may hold values from -0.1875 to 0.1875
- value_weight: bfloat16 [1024, 2048], P(None, 'inner'), may hold values from -0.1875 to 0.1875
- output_weight: bfloat16 [2048, 2048], P('inner'), may hold values from -0.125 to 0.125
- global_latents: bfloat16 [1024, 2048], P(('outer', 'inner')), may hold values from -6 to 6
- decode_query: bfloat16 [2048, 2048], P(None, 'inner'), may hold values from -0.125 to 0.125
- decode_key: bfloat16 [2048, 2048], P(None, 'inner'), may hold values from -0.125 to 0.125
- decode_value: bfloat16 [2048, 2048], P(None, 'inner'), may hold values from -0.125 to 0.125
- decode_output: bfloat16 [2048, 2048], P('inner'), may hold values from -0.125 to 0.125
Outputs:
- decoded: bfloat16 [4096, 2048], P(('outer', 'inner'))
Inputs may be any that keep to these rules, and one draw needn't show every extreme that they name: `slot_ids`: each row holds every slot once.
All inputs are finite; a program needn't handle non-finite values.
Results may differ from a plain program's by a relative error of at most 0.014.
Values may be sent and summed in bfloat16 or wider, within the bound.
No kernel may reach another device: no remote copies, remote signals or barrier semaphores. Data moves between devices by JAX's collectives and lax.ppermute only.
A program may use at most 64 MiB of HBM per device.

v0:
```python
import jax
import jax.numpy as jnp
from jax import lax
from jax.sharding import Mesh
from jax.sharding import PartitionSpec as P

HEAD = 128
INNER = ("inner_0", "inner_1")
OUTER_INNER = ("outer", "inner_0", "inner_1")


def laid_out(tiles, dim):
    shape = list(tiles.shape[1:])
    shape[dim] *= tiles.shape[0]
    return jnp.moveaxis(tiles, 0, dim).reshape(shape)


def stacked_from(value, axes, order):
    tiles = value[None]
    for k in order:
        tiles = lax.all_gather(tiles, axes[k], axis=0, tiled=True)
    carried = [lax.axis_size(axes[k]) for k in reversed(order)]
    tiles = tiles.reshape(*carried, *value.shape)
    turned = sorted(range(len(order)), key=lambda place: order[len(order) - 1 - place])
    return tiles.transpose(*turned, *range(len(order), tiles.ndim)).reshape(-1, *value.shape)


def whole_of(value, axes, order, dim):
    return laid_out(stacked_from(value, axes, order), dim)


def filled_up(lines, size):
    spare = -len(lines) % size
    return jnp.pad(lines, [(0, spare)] + [(0, 0)] * (lines.ndim - 1))


def sum_in_two_steps(value, axis):
    lines = value.reshape(-1, *value.shape[1:][-1:])
    padded = filled_up(lines, lax.axis_size(axis))
    own = lax.psum_scatter(padded, axis, scatter_dimension=0, tiled=True)
    whole = lax.all_gather(own, axis, axis=0, tiled=True)
    return whole[: len(lines)].reshape(value.shape)


def copy_for_each(value, axis):
    copies = jnp.broadcast_to(value, (lax.axis_size(axis), *value.shape))
    return lax.all_to_all(copies, axis, split_axis=0, concat_axis=0, tiled=True)


def gather_directly(value, axis, dim):
    return laid_out(copy_for_each(value, axis), dim)


def in_blocks(value, dim, size):
    before, after = (value.shape[:dim], value.shape[dim + 1 :])
    return jnp.moveaxis(value.reshape(*before, size, -1, *after), dim, 0)


def sent_and_summed(value, axis, dim):
    tiles = in_blocks(value, dim, lax.axis_size(axis))
    arrived = lax.all_to_all(tiles, axis, split_axis=0, concat_axis=0, tiled=True)
    return arrived.astype(jnp.float32).sum(axis=0)


def attend(query_rows, key_rows, value_rows):
    length = query_rows.shape[0]
    head_count = query_rows.shape[1] // HEAD
    queries = query_rows.reshape(length, head_count, HEAD)
    keys_in = key_rows.reshape(key_rows.shape[0], head_count, HEAD)
    values_in = value_rows.reshape(value_rows.shape[0], head_count, HEAD)
    scores = jnp.einsum(
        "qhd,khd->hqk", queries, keys_in, preferred_element_type=jnp.float32
    ) * HEAD ** (-0.5)
    weights = jax.nn.softmax(scores, axis=-1).astype(jnp.bfloat16)
    mixed = jnp.einsum("hqk,khd->qhd", weights, values_in, preferred_element_type=jnp.float32)
    return mixed.reshape(length, head_count * HEAD).astype(jnp.bfloat16)


def local(
    group_latents,
    slot_ids,
    slot_embed,
    merge_latents,
    query_weight,
    key_weight,
    value_weight,
    output_weight,
    global_latents,
    decode_query,
    decode_key,
    decode_value,
    decode_output,
):
    columns = query_weight.shape[1]
    selector = (jnp.arange(slot_embed.shape[0], dtype=jnp.int32) == slot_ids[0, 0]).astype(
        jnp.bfloat16
    )
    slot_vector = jnp.dot(selector[None, :], slot_embed, preferred_element_type=jnp.float32)
    keyed = (group_latents.astype(jnp.float32) + slot_vector).astype(jnp.bfloat16)
    pair_two = jnp.concatenate([key_weight, value_weight], axis=1)
    keys_values = jnp.dot(
        whole_of(keyed, INNER, (0, 1), 0), pair_two, preferred_element_type=jnp.float32
    ).astype(jnp.bfloat16)
    query_two = jnp.dot(merge_latents, query_weight, preferred_element_type=jnp.float32).astype(
        jnp.bfloat16
    )
    mixed_two = attend(query_two, keys_values[:, :columns], keys_values[:, columns:])
    partial_value = jnp.dot(mixed_two, output_weight, preferred_element_type=jnp.float32)
    level_two = merge_latents.astype(jnp.float32) + sum_in_two_steps(
        partial_value.astype(jnp.bfloat16), INNER
    ).astype(jnp.float32)
    normed = (
        level_two * lax.rsqrt(jnp.mean(level_two * level_two, axis=-1, keepdims=True) + 1e-06)
    ).astype(jnp.bfloat16)
    query_five = jnp.dot(normed, decode_query, preferred_element_type=jnp.float32).astype(
        jnp.bfloat16
    )
    pair_five = jnp.concatenate([decode_key, decode_value], axis=1)
    outer_block = gather_directly(global_latents, INNER, 0)
    global_pairs = gather_directly(
        jnp.dot(outer_block, pair_five, preferred_element_type=jnp.float32).astype(jnp.bfloat16),
        "outer",
        0,
    )
    mixed_five = attend(query_five, global_pairs[:, :columns], global_pairs[:, columns:])
    own_rows = merge_latents.shape[0] // lax.axis_size(INNER)
    summed = sent_and_summed(
        jnp.dot(mixed_five, decode_output, preferred_element_type=jnp.float32).astype(jnp.bfloat16),
        INNER,
        0,
    )
    own_part = lax.dynamic_slice_in_dim(level_two, lax.axis_index(INNER) * own_rows, own_rows, 0)
    return (own_part + summed).astype(jnp.bfloat16)


def solution(mesh):
    finer = Mesh(mesh.devices.reshape(mesh.shape["outer"], 4, 4), ("outer", "inner_0", "inner_1"))
    placed = (
        P(OUTER_INNER, None),
        P("outer", INNER),
        P(),
        P(),
        P(None, INNER),
        P(None, INNER),
        P(None, INNER),
        P(INNER, None),
        P(OUTER_INNER, None),
        P(None, INNER),
        P(None, INNER),
        P(None, INNER),
        P(INNER, None),
    )
    return jax.shard_map(
        local, mesh=finer, in_specs=placed, out_specs=P(OUTER_INNER, None), check_vma=False
    )
```

profile of v0, /device:TPU:2, one launch (start us, length us, event | category | flops | bytes accessed | tf_op | source)
XLA Modules:
  0.0 278.3 jit_solution(5552912724020188070)
XLA Ops:
  6.5 0.0 copy-start
  6.5 0.0 all-gather.6.cloned.1.call-start
  7.2 0.9 fusion.28
  8.1 1.7 add_convert_fusion
  9.8 0.0 all-gather.6.cloned.1.call-update
  9.8 0.0 all-gather.4.cloned.1.call-start
  9.9 43.3 %all-gather.6.cloned.1.call-done = bf16[512,1024]{1,0:T(8,128)(2,1)} async-done(((bf16[128,1024]{1,0:T(8,128)(2,1)}), bf16[512,1024]{1,0:T(8,128)(2,1)}) %all-gather.6.cloned.1.call-update) | async-done | bytes 1048592 | tf_op jit(solution)/shard_map/all_gather | solution.py:21
  53.2 0.0 all-gather.4.cloned.1.call-update
  53.2 0.8 broadcast_in_dim.7
  53.9 12.5 %all_to_all.15 = bf16[16,2,2048]{2,1,0:T(2,128)(2,1)S(1)} all-to-all(bf16[16,2,2048]{2,1,0:T(2,128)(2,1)S(1)} %broadcast_in_dim.7), channel_id=1, replica_groups=mesh['outer'=32,'inner_0'=4,'inner_1'=4] {'inner_0','inner_1'}, dimensions={0} | all-to-all | bytes 262144 | tf_op jit(solution)/shard_map/all_to_all | solution.py:47
  66.5 0.1 reshape.87
  66.5 1.5 fusion.3
  68.0 0.9 broadcast_in_dim.8
  68.9 14.9 %all-to-all-start.1 = ((bf16[32,32,256]{2,1,0:T(8,128)(2,1)}), bf16[32,32,256]{2,1,0:T(8,128)(2,1)}, u32[]{:S(2)}, u32[]{:S(2)}) async-start(bf16[32,32,256]{2,1,0:T(8,128)(2,1)} %broadcast_in_dim.8), calls=%async_computation.2 | async-start | bytes 1048576 | tf_op jit(solution)/shard_map/all_to_all | solution.py:47
  83.8 0.0 reduce-scatter.2.cloned.1.call-start
  83.8 25.6 %all-gather.4.cloned.1.call-done = bf16[16,128,1024]{2,1,0:T(8,128)(2,1)} async-done(((bf16[4,128,1024]{2,1,0:T(8,128)(2,1)}), bf16[16,128,1024]{2,1,0:T(8,128)(2,1)}) %all-gather.4.cloned.1.call-update) | async-done | bytes 4194320 | tf_op jit(solution)/shard_map/all_gather | solution.py:21
  109.5 0.0 copy-start.2
  109.5 0.0 copy-start.3
  109.5 2.7 copy.15
  112.2 0.0 copy-start.1
  112.2 0.0 copy-done.2
  112.2 0.0 copy-done.3
  112.2 1.3 convolution_convert_fusion
  113.5 0.0 copy-done
  113.5 0.0 copy-done.1
  113.5 0.6 fusion.35
  114.1 0.3 fusion.7
  114.4 2.8 convolution_convert_fusion.2
  117.2 0.0 reduce-scatter.2.cloned.1.call-update
  117.2 87.4 %reduce-scatter.2.cloned.1.call-done = bf16[8,2048]{1,0:T(8,128)(2,1)} async-done(((bf16[128,2048]{1,0:T(8,128)(2,1)}), bf16[8,2048]{1,0:T(8,128)(2,1)}) %reduce-scatter.2.cloned.1.call-update) | async-done | bytes 32784 | tf_op jit(solution)/shard_map/reduce_scatter | solution.py:40
  204.6 44.8 %all_gather.11 = bf16[128,2048]{1,0:T(8,128)(2,1)S(1)} all-gather(bf16[8,2048]{1,0:T(8,128)(2,1)} %reduce-scatter.2.cloned.1.call-done), channel_id=1, replica_groups=mesh['outer'=32,'inner_0'=4,'inner_1'=4] {'inner_0','inner_1'}, dimensions={0}, use_global_device_ids=true | all-gather | bytes 557056 | tf_op jit(solution)/shard_map/all_gather | solution.py:41
  249.3 0.3 convert_add_fusion
  249.6 0.0 all-to-all-done.1
  249.6 1.7 fusion.36
  251.4 0.2 fusion.20
  251.6 2.7 fusion
  254.3 5.8 %all-to-all-start.2 = ((bf16[16,8,2048]{2,1,0:T(8,128)(2,1)}), bf16[16,8,2048]{2,1,0:T(8,128)(2,1)S(1)}, u32[]{:S(2)}, u32[]{:S(2)}) async-start(bf16[16,8,2048]{2,1,0:T(8,128)(2,1)} %fusion), calls=%async_computation.3 | async-start | bytes 1048576 | tf_op jit(solution)/shard_map/all_to_all | solution.py:61
  260.1 11.0 %all-to-all-done.2 = bf16[16,8,2048]{2,1,0:T(8,128)(2,1)S(1)} async-done(((bf16[16,8,2048]{2,1,0:T(8,128)(2,1)}), bf16[16,8,2048]{2,1,0:T(8,128)(2,1)S(1)}, u32[]{:S(2)}, u32[]{:S(2)}) %all-to-all-start.2) | async-done | bytes 524320 | tf_op jit(solution)/shard_map/all_to_all | solution.py:61
  271.1 0.1 convert_reduce_fusion
  271.2 0.6 add_convert_fusion.1
  (1 shorter events, 0.0 us)
Async XLA Ops:
  6.5 106.9 %copy-start = (bf16[2048,128]{1,0:T(8,128)(2,1)S(1)}, bf16[2048,128]{1,0:T(8,128)(2,1)}, u32[]{:S(2)}) copy-start(bf16[2048,128]{1,0:T(8,128)(2,1)} %param.17) | copy-start | bytes 1572868
  6.5 46.6 %all-gather.6.cloned.1.call-start = ((), (), s32[]{:S(2)}) async-start(), calls=%async_computation.6 | async-start | bytes 1310720 | tf_op jit(solution)/shard_map/all_gather | solution.py:21
  9.8 99.6 %all-gather.4.cloned.1.call-start = ((), (), s32[]{:S(2)}) async-start(), calls=%async_computation.4 | async-start | bytes 5242880 | tf_op jit(solution)/shard_map/all_gather | solution.py:21
  68.9 180.7 %all-to-all-start.1 = ((bf16[32,32,256]{2,1,0:T(8,128)(2,1)}), bf16[32,32,256]{2,1,0:T(8,128)(2,1)}, u32[]{:S(2)}, u32[]{:S(2)}) async-start(bf16[32,32,256]{2,1,0:T(8,128)(2,1)} %broadcast_in_dim.8), calls=%async_computation.2 | async-start | bytes 1048576 | tf_op jit(solution)/shard_map/all_to_all | solution.py:47
  83.8 120.8 %reduce-scatter.2.cloned.1.call-start = ((), (), s32[]{:S(2)}) async-start(), calls=%async_computation.5 | async-start | bytes 557056 | tf_op jit(solution)/shard_map/reduce_scatter | solution.py:40
  109.5 2.7 copy-start.2
  109.5 2.7 copy-start.3
  112.2 1.3 copy-start.1
  254.3 16.8 %all-to-all-start.2 = ((bf16[16,8,2048]{2,1,0:T(8,128)(2,1)}), bf16[16,8,2048]{2,1,0:T(8,128)(2,1)S(1)}, u32[]{:S(2)}, u32[]{:S(2)}) async-start(bf16[16,8,2048]{2,1,0:T(8,128)(2,1)} %fusion), calls=%async_computation.3 | async-start | bytes 1048576 | tf_op jit(solution)/shard_map/all_to_all | solution.py:61
Sparse Core Ops, SparseCore 0:
  10.0 43.1 all-gather.5
  55.2 54.1 all-gather.3
  117.3 87.2 reduce-scatter.1
where the time goes:
time: 279 us; the launch traced here: 278 us
  waiting for transfers between devices  167 us (60%)
  blocking collectives  57.3 us (21%)
  starting transfers between devices  20.8 us (7%)
  between operations  13.9 us (5%)
  matrix products  11.4 us (4%)
  local copies, waits for them, and re-layouts  4.41 us (2%)
  other arithmetic  3.21 us (1%)
    reduce_scatter x1, waiting for transfers between devices, sum_in_two_steps(): own = lax.psum_scatter(padded, axis, scatter_dimension=0, tiled=True)  87.4 us
    all_gather x2, waiting for transfers between devices, stacked_from(): tiles = lax.all_gather(tiles, axes[k], axis=0, tiled=True)  68.9 us
    all_gather x1, blocking collectives, sum_in_two_steps(): whole = lax.all_gather(own, axis, axis=0, tiled=True)  44.8 us
    all_to_all x1, starting transfers between devices, copy_for_each(): return lax.all_to_all(copies, axis, split_axis=0, concat_axis=0, tiled=True)  14.9 us
    all_to_all x1, blocking collectives, copy_for_each(): return lax.all_to_all(copies, axis, split_axis=0, concat_axis=0, tiled=True)  12.5 us
    all_to_all x1, waiting for transfers between devices, sent_and_summed(): lax.all_to_all(tiles, axis, split_axis=0, concat_axis=0, tiled=True)  11 us
    all_to_all x1, starting transfers between devices, sent_and_summed(): lax.all_to_all(tiles, axis, split_axis=0, concat_axis=0, tiled=True)  5.83 us
  transfers between devices with their start and end apart: 5, of which 4 were waited for; matrix products, arithmetic and copies ran while one was open for 4% of the time, Pallas kernels for 0%

commit v1 on v0

--- a/solution.py
+++ b/solution.py
@@ -38,7 +38,9 @@
     lines = value.reshape(-1, *value.shape[1:][-1:])
     padded = filled_up(lines, lax.axis_size(axis))
     own = lax.psum_scatter(padded, axis, scatter_dimension=0, tiled=True)
-    whole = lax.all_gather(own, axis, axis=0, tiled=True)
+    whole = jnp.concatenate(
+        lax.all_to_all(jnp.stack([own] * lax.axis_size(axis)), axis, 0, 0), axis=0
+    )
     return whole[: len(lines)].reshape(value.shape)
 
 

time: 279 us -> 306 us (1.097)
  the two profiles are of different devices: /device:TPU:2 before, /device:TPU:32 now
where the time goes in v1:
time: 306 us; the launch traced here: 305 us
  waiting for transfers between devices  227 us (74%)
  starting transfers between devices  30.3 us (10%)
  between operations  13.9 us (5%)
  blocking collectives  13.5 us (4%)
  matrix products  11.4 us (4%)
  local copies, waits for them, and re-layouts  6.07 us (2%)
  other arithmetic  3.21 us (1%)
    all_gather x2, waiting for transfers between devices, stacked_from(): tiles = lax.all_gather(tiles, axes[k], axis=0, tiled=True)  99.8 us
    reduce_scatter x1, waiting for transfers between devices, sum_in_two_steps(): own = lax.psum_scatter(padded, axis, scatter_dimension=0, tiled=True)  70.1 us
    all_to_all x1, waiting for transfers between devices, copy_for_each(): return lax.all_to_all(copies, axis, split_axis=0, concat_axis=0, tiled=True)  33.6 us
    all_to_all x1, waiting for transfers between devices, sent_and_summed(): lax.all_to_all(tiles, axis, split_axis=0, concat_axis=0, tiled=True)  14.6 us
    all_to_all x1, blocking collectives, copy_for_each(): return lax.all_to_all(copies, axis, split_axis=0, concat_axis=0, tiled=True)  13.5 us
    all_to_all x1, starting transfers between devices, copy_for_each(): return lax.all_to_all(copies, axis, split_axis=0, concat_axis=0, tiled=True)  13.2 us
    all_to_all x1, starting transfers between devices, sum_in_two_steps(): lax.all_to_all(jnp.stack([own] * lax.axis_size(axis)), axis, 0, 0)  11.3 us
    all_to_all x1, waiting for transfers between devices, sum_in_two_steps(): lax.all_to_all(jnp.stack([own] * lax.axis_size(axis)), axis, 0, 0)  8.75 us
  transfers between devices with their start and end apart: 6, of which 6 were waited for; matrix products, arithmetic and copies ran while one was open for 1% of the time, Pallas kernels for 0%

profile of v1, /device:TPU:32, one launch (start us, length us, event | category | flops | bytes accessed | tf_op | source)
XLA Modules:
  0.0 305.3 jit_solution(3006097944056025172)
XLA Ops:
  6.5 0.0 copy-start
  6.5 0.0 all-gather.6.cloned.1.call-start
  7.2 0.9 fusion.28
  8.1 1.7 add_convert_fusion
  9.8 0.0 all-gather.6.cloned.1.call-update
  9.8 0.0 all-gather.4.cloned.1.call-start
  9.9 40.9 %all-gather.6.cloned.1.call-done = bf16[512,1024]{1,0:T(8,128)(2,1)} async-done(((bf16[128,1024]{1,0:T(8,128)(2,1)}), bf16[512,1024]{1,0:T(8,128)(2,1)}) %all-gather.6.cloned.1.call-update) | async-done | bytes 1048592 | tf_op jit(solution)/shard_map/all_gather | solution.py:21
  50.8 0.0 all-gather.4.cloned.1.call-update
  50.8 0.0 reduce-scatter.2.cloned.1.call-start
  50.9 58.9 %all-gather.4.cloned.1.call-done = bf16[16,128,1024]{2,1,0:T(8,128)(2,1)} async-done(((bf16[4,128,1024]{2,1,0:T(8,128)(2,1)}), bf16[16,128,1024]{2,1,0:T(8,128)(2,1)}) %all-gather.4.cloned.1.call-update) | async-done | bytes 4194320 | tf_op jit(solution)/shard_map/all_gather | solution.py:21
  109.7 0.0 copy-start.4
  109.7 0.0 copy-start.5
  109.7 2.7 copy.15
  112.4 0.0 copy-start.1
  112.4 0.0 copy-done.4
  112.5 0.0 copy-done.5
  112.5 1.3 convolution_convert_fusion
  113.7 0.0 copy-done
  113.8 0.0 copy-done.1
  113.8 0.0 copy-start.3
  113.8 0.6 fusion.35
  114.4 0.3 fusion.7
  114.7 2.8 convolution_convert_fusion.2
  117.5 0.0 reduce-scatter.2.cloned.1.call-update
  117.5 0.0 copy-done.3
  117.5 0.1 broadcast_in_dim.7
  117.6 13.5 %all_to_all.20 = bf16[16,2,2048]{2,1,0:T(2,128)(2,1)S(1)} all-to-all(bf16[16,2,2048]{2,1,0:T(2,128)(2,1)S(1)} %broadcast_in_dim.7), channel_id=1, replica_groups=mesh['outer'=32,'inner_0'=4,'inner_1'=4] {'inner_0','inner_1'}, dimensions={0} | all-to-all | bytes 262144 | tf_op jit(solution)/shard_map/all_to_all | solution.py:49
  131.1 70.1 %reduce-scatter.2.cloned.1.call-done = bf16[8,2048]{1,0:T(8,128)(2,1)} async-done(((bf16[128,2048]{1,0:T(8,128)(2,1)}), bf16[8,2048]{1,0:T(8,128)(2,1)}) %reduce-scatter.2.cloned.1.call-update) | async-done | bytes 32784 | tf_op jit(solution)/shard_map/reduce_scatter | solution.py:40
  201.2 1.6 stack.2
  202.8 11.3 %all-to-all-start = ((bf16[16,8,2048]{2,1,0:T(8,128)(2,1)}), bf16[16,8,2048]{2,1,0:T(8,128)(2,1)S(1)}, u32[]{:S(2)}, u32[]{:S(2)}) async-start(bf16[16,8,2048]{2,1,0:T(8,128)(2,1)} %stack.2), calls=%async_computation.1 | async-start | bytes 1048576 | tf_op jit(solution)/shard_map/all_to_all | solution.py:42
  214.1 0.1 reshape.92
  214.2 1.5 fusion.3
  215.7 8.8 %all-to-all-done = bf16[16,8,2048]{2,1,0:T(8,128)(2,1)S(1)} async-done(((bf16[16,8,2048]{2,1,0:T(8,128)(2,1)}), bf16[16,8,2048]{2,1,0:T(8,128)(2,1)S(1)}, u32[]{:S(2)}, u32[]{:S(2)}) %all-to-all-start) | async-done | bytes 524320 | tf_op jit(solution)/shard_map/all_to_all | solution.py:42
  224.4 0.8 broadcast_in_dim.8
  225.3 13.2 %all-to-all-start.2 = ((bf16[32,32,256]{2,1,0:T(8,128)(2,1)}), bf16[32,32,256]{2,1,0:T(8,128)(2,1)S(1)}, u32[]{:S(2)}, u32[]{:S(2)}) async-start(bf16[32,32,256]{2,1,0:T(8,128)(2,1)} %broadcast_in_dim.8), calls=%async_computation.3 | async-start | bytes 1048576 | tf_op jit(solution)/shard_map/all_to_all | solution.py:49
  238.5 0.3 convert_add_fusion
  238.8 33.6 %all-to-all-done.2 = bf16[32,32,256]{2,1,0:T(8,128)(2,1)S(1)} async-done(((bf16[32,32,256]{2,1,0:T(8,128)(2,1)}), bf16[32,32,256]{2,1,0:T(8,128)(2,1)S(1)}, u32[]{:S(2)}, u32[]{:S(2)}) %all-to-all-start.2) | async-done | bytes 524320 | tf_op jit(solution)/shard_map/all_to_all | solution.py:49
  272.4 0.0 copy-start.2
  272.4 0.8 copy-done.2
  273.2 1.7 fusion.36
  274.9 0.2 fusion.20
  275.1 2.7 fusion
  277.8 5.7 %all-to-all-start.3 = ((bf16[16,8,2048]{2,1,0:T(8,128)(2,1)}), bf16[16,8,2048]{2,1,0:T(8,128)(2,1)S(1)}, u32[]{:S(2)}, u32[]{:S(2)}) async-start(bf16[16,8,2048]{2,1,0:T(8,128)(2,1)} %fusion), calls=%async_computation.4 | async-start | bytes 1048576 | tf_op jit(solution)/shard_map/all_to_all | solution.py:63
  283.4 14.6 %all-to-all-done.3 = bf16[16,8,2048]{2,1,0:T(8,128)(2,1)S(1)} async-done(((bf16[16,8,2048]{2,1,0:T(8,128)(2,1)}), bf16[16,8,2048]{2,1,0:T(8,128)(2,1)S(1)}, u32[]{:S(2)}, u32[]{:S(2)}) %all-to-all-start.3) | async-done | bytes 524320 | tf_op jit(solution)/shard_map/all_to_all | solution.py:63
  298.0 0.1 convert_reduce_fusion
  298.1 0.6 add_convert_fusion.1
  (1 shorter events, 0.0 us)
Async XLA Ops:
  6.5 107.2 %copy-start = (bf16[2048,128]{1,0:T(8,128)(2,1)S(1)}, bf16[2048,128]{1,0:T(8,128)(2,1)}, u32[]{:S(2)}) copy-start(bf16[2048,128]{1,0:T(8,128)(2,1)} %param.17) | copy-start | bytes 1572868
  6.5 44.3 %all-gather.6.cloned.1.call-start = ((), (), s32[]{:S(2)}) async-start(), calls=%async_computation.7 | async-start | bytes 1310720 | tf_op jit(solution)/shard_map/all_gather | solution.py:21
  9.8 99.9 %all-gather.4.cloned.1.call-start = ((), (), s32[]{:S(2)}) async-start(), calls=%async_computation.5 | async-start | bytes 5242880 | tf_op jit(solution)/shard_map/all_gather | solution.py:21
  50.8 150.4 %reduce-scatter.2.cloned.1.call-start = ((), (), s32[]{:S(2)}) async-start(), calls=%async_computation.6 | async-start | bytes 557056 | tf_op jit(solution)/shard_map/reduce_scatter | solution.py:40
  109.7 2.7 copy-start.4
  109.7 2.7 copy-start.5
  112.4 1.3 copy-start.1
  113.8 3.7 %copy-start.3 = (bf16[2,2048]{1,0:T(2,128)(2,1)S(1)}, bf16[2,2048]{1,0:T(2,128)(2,1)}, u32[]{:S(2)}) copy-start(bf16[2,2048]{1,0:T(2,128)(2,1)} %param.21) | copy-start | bytes 24580
  202.8 21.6 %all-to-all-start = ((bf16[16,8,2048]{2,1,0:T(8,128)(2,1)}), bf16[16,8,2048]{2,1,0:T(8,128)(2,1)S(1)}, u32[]{:S(2)}, u32[]{:S(2)}) async-start(bf16[16,8,2048]{2,1,0:T(8,128)(2,1)} %stack.2), calls=%async_computation.1 | async-start | bytes 1048576 | tf_op jit(solution)/shard_map/all_to_all | solution.py:42
  225.3 47.1 %all-to-all-start.2 = ((bf16[32,32,256]{2,1,0:T(8,128)(2,1)}), bf16[32,32,256]{2,1,0:T(8,128)(2,1)S(1)}, u32[]{:S(2)}, u32[]{:S(2)}) async-start(bf16[32,32,256]{2,1,0:T(8,128)(2,1)} %broadcast_in_dim.8), calls=%async_computation.3 | async-start | bytes 1048576 | tf_op jit(solution)/shard_map/all_to_all | solution.py:49
  272.4 0.8 copy-start.2
  277.8 20.2 %all-to-all-start.3 = ((bf16[16,8,2048]{2,1,0:T(8,128)(2,1)}), bf16[16,8,2048]{2,1,0:T(8,128)(2,1)S(1)}, u32[]{:S(2)}, u32[]{:S(2)}) async-start(bf16[16,8,2048]{2,1,0:T(8,128)(2,1)} %fusion), calls=%async_computation.4 | async-start | bytes 1048576 | tf_op jit(solution)/shard_map/all_to_all | solution.py:63
Sparse Core Ops, SparseCore 0:
  10.0 40.7 all-gather.5
  52.9 56.7 all-gather.3
  117.6 83.5 reduce-scatter.1
